TPU v7x, 32 devices: a 4x4x1 block of a 4x4x8 slice. The times are simulated.
32 devices in a mesh: rep: 1 (over z), sub: 4 (over y), blk: 8 (over x, core).
Axes of the slice: x: 4, y: 4, z: 1, core: 2. Of those that a mesh axis runs over, the one named last changes fastest.
The devices are a block of a 4x4x8 slice.
Arguments:
- ratings: float32 [16384, 8192], P(('rep', 'blk', 'sub'))
- mask: int32 [16384, 8192], P(('rep', 'blk', 'sub'))
- user_init: float32 [16384, 256], P(('rep', 'blk', 'sub'))
- item_init: float32 [8192, 256], P(('rep', 'blk'))
Outputs:
- output 1: float32 [16384, 256], P(('rep', 'blk', 'sub'))
- output 2: float32 [8192, 256], P(('rep', 'blk'))
All inputs are finite; a program needn't handle non-finite values.
Results may differ from a plain program's by a relative error of at most 0.00127679.
Values are sent between devices in bfloat16 or wider.
A program may use at most 768 MiB of HBM per device.

v0:
```python
import math
import jax
import jax.numpy as jnp
from jax import lax
from jax.sharding import PartitionSpec as P

STEPS = 4
EPOCHS = 2
STEP_GAIN = 0.4
DECAY = 0.002


def solution(mesh):
    blk_size = mesh.shape['blk']
    sub_size = mesh.shape['sub']
    row_spec = P(('rep', 'blk', 'sub'), None)
    item_spec = P(('rep', 'blk'), None)
    prev_pairs = [(source_idx, (source_idx - 1) % blk_size) for source_idx in range(blk_size)]

    def local_run(ratings, mask, user_init, item_init):
        users_dev = ratings.shape[0]
        items_dev, factor_dim = item_init.shape
        big_side = max(items_dev, sub_size * users_dev)
        step_size = STEP_GAIN * math.sqrt(factor_dim) / (math.sqrt(big_side) + math.sqrt(factor_dim)) ** 2
        decay_coef = DECAY / step_size
        blk_pos = lax.axis_index('blk')

        def sub_epoch(counter, state):
            user_st, item_st = state
            col_start = ((blk_pos + counter) % blk_size) * items_dev
            rating_now = lax.dynamic_slice_in_dim(ratings, col_start, items_dev, axis=1)
            mask_now = lax.dynamic_slice_in_dim(mask, col_start, items_dev, axis=1) != 0
            for step_idx in range(STEPS):
                user_half = user_st.astype(jnp.bfloat16)
                item_half = item_st.astype(jnp.bfloat16)
                predicted = lax.dot_general(user_half, item_half, (((1,), (1,)), ((), ())), preferred_element_type=jnp.float32)
                err_half = jnp.where(mask_now, predicted - rating_now, 0.0).astype(jnp.bfloat16)
                grad_user = jnp.dot(err_half, item_half, preferred_element_type=jnp.float32) + decay_coef * user_st
                part_item = lax.dot_general(err_half, user_half, (((0,), (0,)), ((), ())), preferred_element_type=jnp.float32)
                grad_item = lax.psum(part_item, 'sub') + decay_coef * item_st
                user_st = user_st - step_size * grad_user
                item_st = item_st - step_size * grad_item
            return user_st, lax.ppermute(item_st, 'blk', prev_pairs)

        return lax.fori_loop(0, EPOCHS * blk_size, sub_epoch, (user_init, item_init))

    return jax.shard_map(local_run, mesh=mesh, in_specs=(row_spec, row_spec, row_spec, item_spec), out_specs=(row_spec, item_spec), check_vma=False)
```

profile of v0, /device:TPU:112, one launch (start us, length us, event | category | flops | bytes accessed | tf_op | source)
XLA Modules:
  0.0 3327.9 jit_solution(6602129101337334962)
XLA Ops:
  9.0 3311.1 %while.17 = (s32[]{:T(128)}, f32[512,256]{1,0:T(8,128)}, f32[1024,256]{1,0:T(8,128)S(1)}, s32[]{:T(128)}, s32[512,8192]{1,0:T(8,128)}, /*index=5*/f32[512,8192]{...) while((s32[]{:T(128)}, f32[512,256]{1,0:T(8,128)}, ...), condition=%wide.region_5.6_spmd, body=%wide.region_0.5_spmd.sunk | while | flops 3240099840 | bytes 100139648 | solution.py:45
  158.4 42.0 %all-reduce.11.cloned.1.call-done = f32[1024,256]{1,0:T(8,128)} async-done(((f32[1024,256]{1,0:T(8,128)}), f32[1024,256]{1,0:T(8,128)}) %all-reduce.11.cloned.1.call-update) | async-done | bytes 1048592 | tf_op jit(solution)/shard_map/while/body/eval_jaxpr/psum | solution.py:40
  365.4 42.0 %all-reduce.11.cloned.1.call-done = f32[1024,256]{1,0:T(8,128)} async-done(((f32[1024,256]{1,0:T(8,128)}), f32[1024,256]{1,0:T(8,128)}) %all-reduce.11.cloned.1.call-update) | async-done | bytes 1048592 | tf_op jit(solution)/shard_map/while/body/eval_jaxpr/psum | solution.py:40
  430.8 41.5 %all-reduce.5.cloned.1.call-done = f32[1024,256]{1,0:T(8,128)} async-done(((f32[1024,256]{1,0:T(8,128)}), f32[1024,256]{1,0:T(8,128)}) %all-reduce.5.cloned.1.call-update) | async-done | bytes 1048592 | tf_op jit(solution)/shard_map/while/body/eval_jaxpr/psum | solution.py:40
  572.3 42.0 %all-reduce.11.cloned.1.call-done = f32[1024,256]{1,0:T(8,128)} async-done(((f32[1024,256]{1,0:T(8,128)}), f32[1024,256]{1,0:T(8,128)}) %all-reduce.11.cloned.1.call-update) | async-done | bytes 1048592 | tf_op jit(solution)/shard_map/while/body/eval_jaxpr/psum | solution.py:40
  779.3 42.0 %all-reduce.11.cloned.1.call-done = f32[1024,256]{1,0:T(8,128)} async-done(((f32[1024,256]{1,0:T(8,128)}), f32[1024,256]{1,0:T(8,128)}) %all-reduce.11.cloned.1.call-update) | async-done | bytes 1048592 | tf_op jit(solution)/shard_map/while/body/eval_jaxpr/psum | solution.py:40
  844.7 41.5 %all-reduce.5.cloned.1.call-done = f32[1024,256]{1,0:T(8,128)} async-done(((f32[1024,256]{1,0:T(8,128)}), f32[1024,256]{1,0:T(8,128)}) %all-reduce.5.cloned.1.call-update) | async-done | bytes 1048592 | tf_op jit(solution)/shard_map/while/body/eval_jaxpr/psum | solution.py:40
  986.3 42.0 %all-reduce.11.cloned.1.call-done = f32[1024,256]{1,0:T(8,128)} async-done(((f32[1024,256]{1,0:T(8,128)}), f32[1024,256]{1,0:T(8,128)}) %all-reduce.11.cloned.1.call-update) | async-done | bytes 1048592 | tf_op jit(solution)/shard_map/while/body/eval_jaxpr/psum | solution.py:40
  1051.7 41.5 %all-reduce.5.cloned.1.call-done = f32[1024,256]{1,0:T(8,128)} async-done(((f32[1024,256]{1,0:T(8,128)}), f32[1024,256]{1,0:T(8,128)}) %all-reduce.5.cloned.1.call-update) | async-done | bytes 1048592 | tf_op jit(solution)/shard_map/while/body/eval_jaxpr/psum | solution.py:40
  1193.3 42.0 %all-reduce.11.cloned.1.call-done = f32[1024,256]{1,0:T(8,128)} async-done(((f32[1024,256]{1,0:T(8,128)}), f32[1024,256]{1,0:T(8,128)}) %all-reduce.11.cloned.1.call-update) | async-done | bytes 1048592 | tf_op jit(solution)/shard_map/while/body/eval_jaxpr/psum | solution.py:40
  1258.7 41.5 %all-reduce.5.cloned.1.call-done = f32[1024,256]{1,0:T(8,128)} async-done(((f32[1024,256]{1,0:T(8,128)}), f32[1024,256]{1,0:T(8,128)}) %all-reduce.5.cloned.1.call-update) | async-done | bytes 1048592 | tf_op jit(solution)/shard_map/while/body/eval_jaxpr/psum | solution.py:40
  1400.2 42.0 %all-reduce.11.cloned.1.call-done = f32[1024,256]{1,0:T(8,128)} async-done(((f32[1024,256]{1,0:T(8,128)}), f32[1024,256]{1,0:T(8,128)}) %all-reduce.11.cloned.1.call-update) | async-done | bytes 1048592 | tf_op jit(solution)/shard_map/while/body/eval_jaxpr/psum | solution.py:40
  1465.6 41.5 %all-reduce.5.cloned.1.call-done = f32[1024,256]{1,0:T(8,128)} async-done(((f32[1024,256]{1,0:T(8,128)}), f32[1024,256]{1,0:T(8,128)}) %all-reduce.5.cloned.1.call-update) | async-done | bytes 1048592 | tf_op jit(solution)/shard_map/while/body/eval_jaxpr/psum | solution.py:40
  1607.2 42.0 %all-reduce.11.cloned.1.call-done = f32[1024,256]{1,0:T(8,128)} async-done(((f32[1024,256]{1,0:T(8,128)}), f32[1024,256]{1,0:T(8,128)}) %all-reduce.11.cloned.1.call-update) | async-done | bytes 1048592 | tf_op jit(solution)/shard_map/while/body/eval_jaxpr/psum | solution.py:40
  1814.2 42.0 %all-reduce.11.cloned.1.call-done = f32[1024,256]{1,0:T(8,128)} async-done(((f32[1024,256]{1,0:T(8,128)}), f32[1024,256]{1,0:T(8,128)}) %all-reduce.11.cloned.1.call-update) | async-done | bytes 1048592 | tf_op jit(solution)/shard_map/while/body/eval_jaxpr/psum | solution.py:40
  1879.6 41.5 %all-reduce.5.cloned.1.call-done = f32[1024,256]{1,0:T(8,128)} async-done(((f32[1024,256]{1,0:T(8,128)}), f32[1024,256]{1,0:T(8,128)}) %all-reduce.5.cloned.1.call-update) | async-done | bytes 1048592 | tf_op jit(solution)/shard_map/while/body/eval_jaxpr/psum | solution.py:40
  2021.1 42.0 %all-reduce.11.cloned.1.call-done = f32[1024,256]{1,0:T(8,128)} async-done(((f32[1024,256]{1,0:T(8,128)}), f32[1024,256]{1,0:T(8,128)}) %all-reduce.11.cloned.1.call-update) | async-done | bytes 1048592 | tf_op jit(solution)/shard_map/while/body/eval_jaxpr/psum | solution.py:40
  2228.1 42.0 %all-reduce.11.cloned.1.call-done = f32[1024,256]{1,0:T(8,128)} async-done(((f32[1024,256]{1,0:T(8,128)}), f32[1024,256]{1,0:T(8,128)}) %all-reduce.11.cloned.1.call-update) | async-done | bytes 1048592 | tf_op jit(solution)/shard_map/while/body/eval_jaxpr/psum | solution.py:40
  2293.5 41.5 %all-reduce.5.cloned.1.call-done = f32[1024,256]{1,0:T(8,128)} async-done(((f32[1024,256]{1,0:T(8,128)}), f32[1024,256]{1,0:T(8,128)}) %all-reduce.5.cloned.1.call-update) | async-done | bytes 1048592 | tf_op jit(solution)/shard_map/while/body/eval_jaxpr/psum | solution.py:40
  2435.1 42.0 %all-reduce.11.cloned.1.call-done = f32[1024,256]{1,0:T(8,128)} async-done(((f32[1024,256]{1,0:T(8,128)}), f32[1024,256]{1,0:T(8,128)}) %all-reduce.11.cloned.1.call-update) | async-done | bytes 1048592 | tf_op jit(solution)/shard_map/while/body/eval_jaxpr/psum | solution.py:40
  2642.1 42.0 %all-reduce.11.cloned.1.call-done = f32[1024,256]{1,0:T(8,128)} async-done(((f32[1024,256]{1,0:T(8,128)}), f32[1024,256]{1,0:T(8,128)}) %all-reduce.11.cloned.1.call-update) | async-done | bytes 1048592 | tf_op jit(solution)/shard_map/while/body/eval_jaxpr/psum | solution.py:40
  2849.0 42.0 %all-reduce.11.cloned.1.call-done = f32[1024,256]{1,0:T(8,128)} async-done(((f32[1024,256]{1,0:T(8,128)}), f32[1024,256]{1,0:T(8,128)}) %all-reduce.11.cloned.1.call-update) | async-done | bytes 1048592 | tf_op jit(solution)/shard_map/while/body/eval_jaxpr/psum | solution.py:40
  3056.0 42.0 %all-reduce.11.cloned.1.call-done = f32[1024,256]{1,0:T(8,128)} async-done(((f32[1024,256]{1,0:T(8,128)}), f32[1024,256]{1,0:T(8,128)}) %all-reduce.11.cloned.1.call-update) | async-done | bytes 1048592 | tf_op jit(solution)/shard_map/while/body/eval_jaxpr/psum | solution.py:40
  3263.0 42.0 %all-reduce.11.cloned.1.call-done = f32[1024,256]{1,0:T(8,128)} async-done(((f32[1024,256]{1,0:T(8,128)}), f32[1024,256]{1,0:T(8,128)}) %all-reduce.11.cloned.1.call-update) | async-done | bytes 1048592 | tf_op jit(solution)/shard_map/while/body/eval_jaxpr/psum | solution.py:40
  (639 shorter events, 2348.6 us)
Async XLA Ops:
  15.7 89.9 %all-reduce.7.cloned.1.call-start = ((), (), s32[]{:S(2)}) async-start(), calls=%async_computation.1 | async-start | bytes 2097152 | tf_op jit(solution)/shard_map/while/body/eval_jaxpr/psum | solution.py:40
  222.2 90.3 %all-reduce.7.cloned.1.call-start = ((), (), s32[]{:S(2)}) async-start(), calls=%async_computation.1 | async-start | bytes 2097152 | tf_op jit(solution)/shard_map/while/body/eval_jaxpr/psum | solution.py:40
  429.2 90.3 %all-reduce.7.cloned.1.call-start = ((), (), s32[]{:S(2)}) async-start(), calls=%async_computation.1 | async-start | bytes 2097152 | tf_op jit(solution)/shard_map/while/body/eval_jaxpr/psum | solution.py:40
  477.5 89.5 %all-reduce.9.cloned.1.call-start = ((), (), s32[]{:S(2)}) async-start(), calls=%async_computation.2 | async-start | bytes 2097152 | tf_op jit(solution)/shard_map/while/body/eval_jaxpr/psum | solution.py:40
  636.2 90.3 %all-reduce.7.cloned.1.call-start = ((), (), s32[]{:S(2)}) async-start(), calls=%async_computation.1 | async-start | bytes 2097152 | tf_op jit(solution)/shard_map/while/body/eval_jaxpr/psum | solution.py:40
  684.5 89.5 %all-reduce.9.cloned.1.call-start = ((), (), s32[]{:S(2)}) async-start(), calls=%async_computation.2 | async-start | bytes 2097152 | tf_op jit(solution)/shard_map/while/body/eval_jaxpr/psum | solution.py:40
  843.1 90.3 %all-reduce.7.cloned.1.call-start = ((), (), s32[]{:S(2)}) async-start(), calls=%async_computation.1 | async-start | bytes 2097152 | tf_op jit(solution)/shard_map/while/body/eval_jaxpr/psum | solution.py:40
  891.5 89.5 %all-reduce.9.cloned.1.call-start = ((), (), s32[]{:S(2)}) async-start(), calls=%async_computation.2 | async-start | bytes 2097152 | tf_op jit(solution)/shard_map/while/body/eval_jaxpr/psum | solution.py:40
  1050.1 90.3 %all-reduce.7.cloned.1.call-start = ((), (), s32[]{:S(2)}) async-start(), calls=%async_computation.1 | async-start | bytes 2097152 | tf_op jit(solution)/shard_map/while/body/eval_jaxpr/psum | solution.py:40
  1098.5 89.5 %all-reduce.9.cloned.1.call-start = ((), (), s32[]{:S(2)}) async-start(), calls=%async_computation.2 | async-start | bytes 2097152 | tf_op jit(solution)/shard_map/while/body/eval_jaxpr/psum | solution.py:40
  1257.1 90.3 %all-reduce.7.cloned.1.call-start = ((), (), s32[]{:S(2)}) async-start(), calls=%async_computation.1 | async-start | bytes 2097152 | tf_op jit(solution)/shard_map/while/body/eval_jaxpr/psum | solution.py:40
  1305.4 89.5 %all-reduce.9.cloned.1.call-start = ((), (), s32[]{:S(2)}) async-start(), calls=%async_computation.2 | async-start | bytes 2097152 | tf_op jit(solution)/shard_map/while/body/eval_jaxpr/psum | solution.py:40
  1464.1 90.3 %all-reduce.7.cloned.1.call-start = ((), (), s32[]{:S(2)}) async-start(), calls=%async_computation.1 | async-start | bytes 2097152 | tf_op jit(solution)/shard_map/while/body/eval_jaxpr/psum | solution.py:40
  1512.4 89.5 %all-reduce.9.cloned.1.call-start = ((), (), s32[]{:S(2)}) async-start(), calls=%async_computation.2 | async-start | bytes 2097152 | tf_op jit(solution)/shard_map/while/body/eval_jaxpr/psum | solution.py:40
  1671.0 90.3 %all-reduce.7.cloned.1.call-start = ((), (), s32[]{:S(2)}) async-start(), calls=%async_computation.1 | async-start | bytes 2097152 | tf_op jit(solution)/shard_map/while/body/eval_jaxpr/psum | solution.py:40
  1719.4 89.5 %all-reduce.9.cloned.1.call-start = ((), (), s32[]{:S(2)}) async-start(), calls=%async_computation.2 | async-start | bytes 2097152 | tf_op jit(solution)/shard_map/while/body/eval_jaxpr/psum | solution.py:40
  1878.0 90.3 %all-reduce.7.cloned.1.call-start = ((), (), s32[]{:S(2)}) async-start(), calls=%async_computation.1 | async-start | bytes 2097152 | tf_op jit(solution)/shard_map/while/body/eval_jaxpr/psum | solution.py:40
  1926.4 89.5 %all-reduce.9.cloned.1.call-start = ((), (), s32[]{:S(2)}) async-start(), calls=%async_computation.2 | async-start | bytes 2097152 | tf_op jit(solution)/shard_map/while/body/eval_jaxpr/psum | solution.py:40
  2085.0 90.3 %all-reduce.7.cloned.1.call-start = ((), (), s32[]{:S(2)}) async-start(), calls=%async_computation.1 | async-start | bytes 2097152 | tf_op jit(solution)/shard_map/while/body/eval_jaxpr/psum | solution.py:40
  2292.0 90.3 %all-reduce.7.cloned.1.call-start = ((), (), s32[]{:S(2)}) async-start(), calls=%async_computation.1 | async-start | bytes 2097152 | tf_op jit(solution)/shard_map/while/body/eval_jaxpr/psum | solution.py:40
  2498.9 90.3 %all-reduce.7.cloned.1.call-start = ((), (), s32[]{:S(2)}) async-start(), calls=%async_computation.1 | async-start | bytes 2097152 | tf_op jit(solution)/shard_map/while/body/eval_jaxpr/psum | solution.py:40
  2705.9 90.3 %all-reduce.7.cloned.1.call-start = ((), (), s32[]{:S(2)}) async-start(), calls=%async_computation.1 | async-start | bytes 2097152 | tf_op jit(solution)/shard_map/while/body/eval_jaxpr/psum | solution.py:40
  2912.9 90.3 %all-reduce.7.cloned.1.call-start = ((), (), s32[]{:S(2)}) async-start(), calls=%async_computation.1 | async-start | bytes 2097152 | tf_op jit(solution)/shard_map/while/body/eval_jaxpr/psum | solution.py:40
  3119.8 90.3 %all-reduce.7.cloned.1.call-start = ((), (), s32[]{:S(2)}) async-start(), calls=%async_computation.1 | async-start | bytes 2097152 | tf_op jit(solution)/shard_map/while/body/eval_jaxpr/psum | solution.py:40
  (138 other events, 5292.7 us)
Sparse Core Ops, SparseCore 0:
  15.8 42.4 all-reduce.4
  222.3 42.9 all-reduce.4
  318.2 41.8 all-reduce.8
  429.3 42.9 all-reduce.4
  525.1 41.8 all-reduce.8
  636.3 42.9 all-reduce.4
  732.1 41.8 all-reduce.8
  843.3 42.9 all-reduce.4
  939.1 41.8 all-reduce.8
  1050.2 42.9 all-reduce.4
  1146.0 41.8 all-reduce.8
  1257.2 42.9 all-reduce.4
  1353.0 41.8 all-reduce.8
  1464.2 42.9 all-reduce.4
  1560.0 41.8 all-reduce.8
  1671.2 42.9 all-reduce.4
  1767.0 41.8 all-reduce.8
  1878.1 42.9 all-reduce.4
  2085.1 42.9 all-reduce.4
  2292.1 42.9 all-reduce.4
  2499.0 42.9 all-reduce.4
  2706.0 42.9 all-reduce.4
  2913.0 42.9 all-reduce.4
  3120.0 42.9 all-reduce.4
  (40 shorter events, 1671.0 us)
where the time goes:
time: 3340 us; the launch traced here: 3330 us
  waiting for transfers between devices  2780 us (83%)
  matrix products  378 us (11%)
  other arithmetic  149 us (4%)
    psum x64, waiting for transfers between devices, sub_epoch(): grad_item = lax.psum(part_item, 'sub') + decay_coef * item_st  2620 us
    ppermute x16, waiting for transfers between devices, sub_epoch(): return (user_st, lax.ppermute(item_st, 'blk', prev_pairs))  157 us
    dot_general x64, matrix products, sub_epoch(): lax.dot_general(user_half, item_half, (((1,), (1,)), ((), ())), preferred...  143 us
    dot_general x64, matrix products, sub_epoch(): jnp.dot(err_half, item_half, preferred_element_type=jnp.float32)  124 us
    dot_general x64, matrix products, sub_epoch(): lax.dot_general(err_half, user_half, (((0,), (0,)), ((), ())), preferred_...  111 us
    sub x32, other arithmetic, sub_epoch(): item_st = item_st - step_size * grad_item  74.4 us
  transfers between devices with their start and end apart: 80, of which 80 were waited for; matrix products, arithmetic and copies ran while one was open for 4% of the time, Pallas kernels for 0%

commit v1 on v0

v1 whole, which is shorter than its diff:
```python
import functools
import math
import jax
import jax.numpy as jnp
from jax import lax
from jax.experimental import pallas as pl
from jax.experimental.pallas import tpu as pltpu
from jax.sharding import PartitionSpec as P

STEPS = 4
EPOCHS = 2
STEP_GAIN = 0.4
DECAY = 0.002
ITEM_CHUNK = 256
USER_CHUNK = 512
F32 = jnp.float32
BF16 = jnp.bfloat16


def kernel(n_sub, n_blk, step_size, decay_coef, ratings, mask, user_in, item_in, user_out, item_out, far_ratings,
           rating_buf, mask_buf, item_st, user_st, user_half, item_half, err_buf,
           own_sem, mask_sem, part_sem, rating_recv, rating_send, fwd_send, user_recv, user_send, item_recv, item_send,
           out_recv, out_send, last_recv, last_send):
    rep, sub, blk = lax.axis_index('rep'), lax.axis_index('sub'), lax.axis_index('blk')
    n = user_in.shape[0]
    half = n // 2
    n_chunks, factor_dim, width = item_in.shape
    items = n_chunks * width
    users = user_st.shape[0]
    n_turns = EPOCHS * n_blk

    def root_of(b):
        return (b // 2 + b) % 2 * (n_sub // 2)

    root = root_of(blk)
    rel = (sub + n_sub - root) % n_sub
    next_blk, prev_blk = (blk + n_blk - 1) % n_blk, (blk + 1) % n_blk
    far = (root + 2) % n_sub
    side = rel // 2

    def remote(src, dst, send_sem, recv_sem, to_sub, to_blk):
        return pltpu.make_async_remote_copy(src_ref=src, dst_ref=dst, send_sem=send_sem, recv_sem=recv_sem,
                                            device_id=(rep, to_sub, to_blk), device_id_type=pl.DeviceIdType.MESH)

    def arrived(dst, recv_sem):
        remote(dst, dst, user_send.at[0], recv_sem, (sub + 1) % n_sub, blk).wait_recv()

    barrier = pltpu.get_barrier_semaphore()
    for d in range(1, n_sub):
        pl.semaphore_signal(barrier, inc=1, device_id=(rep, (sub + d) % n_sub, blk), device_id_type=pl.DeviceIdType.MESH)

    @pl.when(rel == 0)
    def _():
        for b in (next_blk, prev_blk):
            pl.semaphore_signal(barrier, inc=1, device_id=(rep, root_of(b), b), device_id_type=pl.DeviceIdType.MESH)
        pl.semaphore_wait(barrier, n_sub + 1)

    @pl.when(rel != 0)
    def _():
        pl.semaphore_wait(barrier, n_sub - 1)

    def own_copies(t, slot):
        cols = pl.ds(pl.multiple_of((blk + t) % n_blk * items, items), items)
        return (pltpu.make_async_copy(ratings.at[:, cols], rating_buf.at[slot, pl.ds(0, n)], own_sem.at[slot]),
                pltpu.make_async_copy(mask.at[:, cols], mask_buf.at[slot], mask_sem.at[slot]))

    def load_own(t, slot):
        for copy in own_copies(t, slot):
            copy.start()

    def merge_own(t, slot, start):
        for copy in own_copies(t, slot):
            copy.wait()
        rating_buf[slot, pl.ds(start, n)] = jnp.where(mask_buf[slot] != 0, rating_buf[slot, pl.ds(0, n)], jnp.inf)

    def part_rows(k):
        return pl.ds((n, 2 * n, 3 * n, 3 * n + half)[k], (n, n, half, half)[k])

    def far_slice(t, rows):
        return far_ratings.at[t, pl.ds(rows.start - n, rows.size)]

    @pl.when(rel == 2)
    def _():
        load_own(0, 0)
        load_own(1, 1)
        first = [remote(user_in.at[pl.ds(k * half, half)], user_st.at[part_rows(2 + k)], user_send.at[k], user_recv.at[2 + k],
                        (root + 1 + 2 * k) % n_sub, blk) for k in range(2)]
        for copy in first:
            copy.start()

        def sends(t, slot):
            return [remote(rating_buf.at[slot, pl.ds(n + k * half, half)], far_slice(t, part_rows(2 + k)),
                           rating_send.at[slot, k], rating_recv.at[t, 2 + k], (root + 1 + 2 * k) % n_sub, blk) for k in range(2)]

        def turn(t, carry):
            slot = t % 2

            @pl.when(t >= 2)
            def _():
                for copy in sends(t - 2, slot):
                    copy.wait_send()
            merge_own(t, slot, n)
            for copy in sends(t, slot):
                copy.start()

            @pl.when(t + 2 < n_blk)
            def _():
                load_own(t + 2, slot)
            return carry

        lax.fori_loop(0, n_blk, turn, 0)
        for t in (n_blk - 2, n_blk - 1):
            for copy in sends(t, t % 2):
                copy.wait_send()
        for copy in first:
            copy.wait_send()
        for k in range(2):
            arrived(user_out.at[pl.ds(k * half, half)], out_recv.at[k])
        for c in range(n_chunks):
            arrived(item_out.at[c], last_recv.at[c])

    @pl.when((rel == 1) | (rel == 3))
    def _():
        load_own(0, 0)
        load_own(1, 1)
        own_start = pl.multiple_of(n + side * n, n)
        far_start = pl.multiple_of(3 * n + side * half, half)
        own_rows, far_rows = pl.ds(own_start, n), pl.ds(far_start, half)
        mine = remote(user_in, user_st.at[own_rows], user_send.at[0], user_recv.at[side], root, blk)
        mine.start()

        def own_send(t, slot):
            return remote(rating_buf.at[slot, pl.ds(n, n)], far_ratings.at[t, pl.ds(pl.multiple_of(own_start - n, n), n)],
                          rating_send.at[slot, 0], rating_recv.at[t, side], root, blk)

        def far_send(t, slot):
            there = far_ratings.at[t, pl.ds(pl.multiple_of(far_start - n, half), half)]
            return remote(there, there, fwd_send.at[slot], rating_recv.at[t, 2 + side], root, blk)

        arrived(user_st.at[far_rows], user_recv.at[2 + side])
        passed = remote(user_st.at[far_rows], user_st.at[far_rows], user_send.at[1], user_recv.at[2 + side], root, blk)
        passed.start()

        def turn(t, carry):
            slot = t % 2

            @pl.when(t >= 2)
            def _():
                own_send(t - 2, slot).wait_send()
                far_send(t - 2, slot).wait_send()
            merge_own(t, slot, n)
            own_send(t, slot).start()
            far_send(t, slot).wait_recv()
            far_send(t, slot).start()

            @pl.when(t + 2 < n_blk)
            def _():
                load_own(t + 2, slot)
            return carry

        lax.fori_loop(0, n_blk, turn, 0)
        for t in (n_blk - 2, n_blk - 1):
            own_send(t, t % 2).wait_send()
            far_send(t, t % 2).wait_send()
        mine.wait_send()
        passed.wait_send()
        arrived(user_st.at[pl.ds(0, half)], out_recv.at[2])
        back = remote(user_st.at[pl.ds(0, half)], user_out.at[pl.ds(pl.multiple_of(side * half, half), half)], out_send.at[0], out_recv.at[side], far, blk)
        back.start()
        arrived(user_out, out_recv.at[0])
        back_items = []
        for c in range(n_chunks):
            arrived(item_out.at[c], last_recv.at[c])
            copy = remote(item_out.at[c], item_out.at[c], last_send.at[c], last_recv.at[c], far, blk)
            mine_to_pass = side == (2 * c) // n_chunks

            @pl.when(mine_to_pass)
            def _():
                copy.start()
            back_items.append((copy, mine_to_pass))
        for copy, mine_to_pass in back_items:
            @pl.when(mine_to_pass)
            def _():
                copy.wait_send()
        back.wait_send()

    @pl.when(rel == 0)
    def _():
        load_own(0, 0)
        for c in range(n_chunks):
            item_st[0, c] = item_in[c]
        user_st[pl.ds(0, n)] = user_in[...]
        for k in range(4):
            arrived(user_st.at[part_rows(k)], user_recv.at[k])
        user_half[...] = user_st[...].astype(BF16)

        def part_copy(t, slot):
            return pltpu.make_async_copy(far_ratings.at[t % n_blk], rating_buf.at[slot, pl.ds(n, users - n)], part_sem.at[slot])

        def item_copy(t, c):
            return remote(item_st.at[t, c], item_st.at[t + 1, c], item_send.at[c], item_recv.at[t + 1, c], root_of(next_blk), next_blk)

        def step(t, slot, first, last):
            for c in range(n_chunks):
                if first:
                    @pl.when(t > 0)
                    def _():
                        arrived(item_st.at[t, c], item_recv.at[t, c])
                cols = pl.ds(c * width, width)
                item_old = item_st[t, c]
                item_now = item_old.astype(BF16)
                item_half[:, cols] = item_now
                predicted = jnp.dot(user_half[...], item_now, preferred_element_type=F32)
                rating = rating_buf[slot, :, cols]
                err = jnp.where(rating == jnp.inf, 0.0, predicted - rating).astype(BF16)
                err_buf[:, cols] = err
                grad_item = lax.dot_general(user_half[...], err, (((0,), (0,)), ((), ())), preferred_element_type=F32)
                item_st[t, c] = item_old - step_size * (grad_item + decay_coef * item_old)
                if last:
                    item_copy(t, c).start()
            for i in range(users // USER_CHUNK):
                rows = pl.ds(i * USER_CHUNK, USER_CHUNK)
                grad_user = lax.dot_general(err_buf[rows, :], item_half[...], (((1,), (1,)), ((), ())), preferred_element_type=F32)
                user_old = user_st[rows, :]
                user_new = user_old - step_size * (grad_user + decay_coef * user_old)
                user_st[rows, :] = user_new
                user_half[rows, :] = user_new.astype(BF16)

        def turn(t, carry):
            slot = t % 2

            @pl.when(t < n_blk)
            def _():
                for k in range(4):
                    arrived(far_slice(t, part_rows(k)), rating_recv.at[t, k])
                part_copy(t, slot).start()
            merge_own(t, slot, 0)
            part_copy(t, slot).wait()

            @pl.when(t + 1 < n_turns)
            def _():
                load_own(t + 1, 1 - slot)

            @pl.when((t + 1 >= n_blk) & (t + 1 < n_turns))
            def _():
                part_copy(t + 1, 1 - slot).start()
            step(t, slot, True, False)

            def middle(_, c):
                step(t, slot, False, False)
                return c

            lax.fori_loop(0, STEPS - 2, middle, 0)

            @pl.when(t > 0)
            def _():
                for c in range(n_chunks):
                    item_copy(t - 1, c).wait_send()
            step(t, slot, False, True)
            return carry

        lax.fori_loop(0, n_turns, turn, 0)
        outs = []
        for k in range(2):
            to = (root + 1 + 2 * k) % n_sub
            outs.append(remote(user_st.at[part_rows(2 + k)], user_st.at[pl.ds(0, half)], out_send.at[k], out_recv.at[2], to, blk))
        for k in range(2):
            to = (root + 1 + 2 * k) % n_sub
            outs.append(remote(user_st.at[part_rows(k)], user_out, out_send.at[2 + k], out_recv.at[0], to, blk))
        for copy in outs:
            copy.start()
        user_out[...] = user_st[pl.ds(0, n)]
        for c in range(n_chunks):
            arrived(item_st.at[n_turns, c], item_recv.at[n_turns, c])
            for k in range(2):
                to = (root + 1 + 2 * k) % n_sub
                copy = remote(item_st.at[n_turns, c], item_out.at[c], last_send.at[c + k * n_chunks], last_recv.at[c], to, blk)
                copy.start()
                outs.append(copy)
            item_out[c] = item_st[n_turns, c]
        for c in range(n_chunks):
            item_copy(n_turns - 1, c).wait_send()
        for copy in outs:
            copy.wait_send()


def solution(mesh):
    n_sub, n_blk = mesh.shape['sub'], mesh.shape['blk']
    row_spec = P(('rep', 'blk', 'sub'), None)
    item_spec = P(('rep', 'blk'), None)

    def local_run(ratings, mask, user_init, item_init):
        users_dev = ratings.shape[0]
        items_dev, factor_dim = item_init.shape
        users = n_sub * users_dev
        big_side = max(items_dev, users)
        step_size = STEP_GAIN * math.sqrt(factor_dim) / (math.sqrt(big_side) + math.sqrt(factor_dim)) ** 2
        decay_coef = DECAY / step_size
        n_chunks = items_dev // ITEM_CHUNK
        n_turns = EPOCHS * n_blk
        item_parts = item_init.reshape(n_chunks, ITEM_CHUNK, factor_dim).transpose(0, 2, 1)
        hbm, vmem = pl.BlockSpec(memory_space=pltpu.HBM), pl.BlockSpec(memory_space=pltpu.VMEM)
        dma = pltpu.SemaphoreType.DMA
        user_out, item_out, _ = pl.pallas_call(
            functools.partial(kernel, n_sub, n_blk, step_size, decay_coef),
            out_shape=(jax.ShapeDtypeStruct(user_init.shape, F32), jax.ShapeDtypeStruct(item_parts.shape, F32),
                       jax.ShapeDtypeStruct((n_blk, users - users_dev, items_dev), F32)),
            in_specs=[hbm, hbm, vmem, vmem],
            out_specs=(vmem, vmem, hbm),
            scratch_shapes=[
                pltpu.VMEM((2, users, items_dev), F32),
                pltpu.VMEM((2, users_dev, items_dev), jnp.int32),
                pltpu.VMEM((n_turns + 1,) + item_parts.shape, F32),
                pltpu.VMEM((users, factor_dim), F32),
                pltpu.VMEM((users, factor_dim), BF16),
                pltpu.VMEM((factor_dim, items_dev), BF16),
                pltpu.VMEM((users, items_dev), BF16),
                dma((2,)), dma((2,)), dma((2,)), dma((n_blk, 4)), dma((2, 2)), dma((2,)), dma((4,)), dma((2,)),
                dma((n_turns + 1, n_chunks)), dma((n_chunks,)), dma((3,)), dma((4,)), dma((n_chunks,)), dma((2 * n_chunks,)),
            ],
            compiler_params=pltpu.CompilerParams(collective_id=0, has_side_effects=True, vmem_limit_bytes=62 * 2**20),
            name='dsgd',
        )(ratings, mask, user_init, item_parts)
        return user_out, item_out.transpose(0, 2, 1).reshape(items_dev, factor_dim)

    return jax.shard_map(local_run, mesh=mesh, in_specs=(row_spec, row_spec, row_spec, item_spec), out_specs=(row_spec, item_spec), check_vma=False)
```

time: 3340 us -> 614 us (0.18)
  waiting for transfers between devices: 2780 us -> 0 us
  Pallas kernels: 0 us -> 605 us
  matrix products: 378 us -> 0 us
  other arithmetic: 149 us -> 0 us
    psum x64 -> x0, waiting for transfers between devices: 2620 us -> none  [sub_epoch(): grad_item = lax.psum(part_item, 'sub') + decay_coef * item_st]
    pallas_call x0 -> x1, Pallas kernels: none -> 605 us  [local_run(): pl.pallas_call(functools.partial(kernel, n_sub, n_blk, step_size, decay_c...]
    dot_general x192 -> x0, matrix products: 378 us -> none  [the longest x64 143 us: sub_epoch(): lax.dot_general(user_half, item_half, (((1,), (1,)), ((), ())), preferred...]
    ppermute x16 -> x0, waiting for transfers between devices: 157 us -> none  [sub_epoch(): return (user_st, lax.ppermute(item_st, 'blk', prev_pairs))]
    sub x32 -> x0, other arithmetic: 74.4 us -> none  [sub_epoch(): item_st = item_st - step_size * grad_item]
    convert_element_type x32 -> x0, other arithmetic: 44.9 us -> none  [sub_epoch(): item_half = item_st.astype(jnp.bfloat16)]
  transfers between devices with their start and end apart: 80 -> 0, of which waited for: 80 -> 0; matrix products, arithmetic and copies ran while one was open for 4% -> 0% of each run, Pallas kernels for 0% -> 0%
where the time goes in v1:
time: 614 us; the launch traced here: 612 us
  Pallas kernels  605 us (99%)
  local copies, waits for them, and re-layouts  6.93 us (1%)
    pallas_call x1, Pallas kernels, local_run(): pl.pallas_call(functools.partial(kernel, n_sub, n_blk, step_size, decay_c...  605 us

profile of v1, /device:TPU:112, one launch (start us, length us, event | category | flops | bytes accessed | tf_op | source)
XLA Modules:
  0.0 612.2 jit_solution(10164180919377901695)
XLA Ops:
  0.6 2.5 copy.6
  3.2 604.6 %dsgd.1 = (f32[512,256]{1,0:T(8,128)}, f32[4,256,256]{2,1,0:T(8,128)}, f32[8,1536,1024]{2,1,0:T(8,128)}) custom-call(f32[512,8192]{1,0:T(8,128)} %ratings.1, s32[512,8192]{1,0:T(8,128)} %mask.1, f32[512,256]{1,0:T(8,128)} %user_in.1, f32[4,256,256]{2,1,0:T(8,128)} %bitcast.4), custom_call_target="tpu_custom_call" | custom-call | tf_op jit(solution)/shard_map/dsgd/pallas_call | solution.py:304
  607.8 2.5 copy.7
  610.3 1.9 copy.9

commit v2 on v1

v2 whole, which is shorter than its diff:
```python
import functools
import math
import jax
import jax.numpy as jnp
from jax import lax
from jax.experimental import pallas as pl
from jax.experimental.pallas import tpu as pltpu
from jax.sharding import PartitionSpec as P

STEPS = 4
EPOCHS = 2
STEP_GAIN = 0.4
DECAY = 0.002
ITEM_CHUNK = 256
USER_CHUNK = 512
PARTS = 2
DEPTH = 4
LAG = 1
F32 = jnp.float32
BF16 = jnp.bfloat16


def kernel(n_sub, n_blk, step_size, decay_coef, ratings, mask, user_in, item_in, user_out, item_out, far_ratings,
           rating_buf, mask_buf, item_st, user_st, user_half, item_half, err_buf,
           own_sem, mask_sem, part_sem, rating_recv, far_recv, relay_recv, rating_send, fwd_send, relay_sem, user_recv, user_send, item_recv, item_send,
           out_recv, out_send, last_recv, last_send):
    rep, sub, blk = lax.axis_index('rep'), lax.axis_index('sub'), lax.axis_index('blk')
    n_dev = user_in.shape[0]
    n = n_dev // PARTS
    half = n // 2
    n_chunks, factor_dim, width = item_in.shape
    items = n_chunks * width
    users = user_st.shape[0]
    n_turns = EPOCHS * n_blk

    def root_of(b):
        return b // 2 % 2 + b % 2 * (n_sub // 2)

    root = root_of(blk)
    rel = (sub + n_sub - root) % n_sub
    next_blk, prev_blk = (blk + n_blk - 1) % n_blk, (blk + 1) % n_blk
    side = rel // 2
    col = blk // 2
    n_cols = n_blk // 2
    twin, twin_from = (col + 1) % n_cols, (col + n_cols - 1) % n_cols
    region = n + half
    hot = (side + col) % 2 == 1
    direct_hot, direct_cold = n, n + half // 2

    def side_sub(k):
        return (root + 1 + 2 * k) % n_sub

    def relay_of(k):
        return 2 * twin + (root + 2 * n_sub - twin % 2 - 1 - 2 * k) % n_sub // 2

    twin_blk = 2 * twin_from + (sub + n_sub - twin_from % 2) % n_sub // 2

    def remote(src, dst, send_sem, recv_sem, to_sub, to_blk):
        return pltpu.make_async_remote_copy(src_ref=src, dst_ref=dst, send_sem=send_sem, recv_sem=recv_sem,
                                            device_id=(rep, to_sub, to_blk), device_id_type=pl.DeviceIdType.MESH)

    def arrived(dst, recv_sem):
        remote(dst, dst, user_send.at[0], recv_sem, (sub + 1) % n_sub, blk).wait_recv()

    barrier = pltpu.get_barrier_semaphore()

    def greet(to_sub, to_blk):
        pl.semaphore_signal(barrier, inc=1, device_id=(rep, to_sub, to_blk), device_id_type=pl.DeviceIdType.MESH)

    for d in range(1, n_sub):
        greet((sub + d) % n_sub, blk)

    @pl.when(rel == 0)
    def _():
        for b in (next_blk, prev_blk):
            greet(root_of(b), b)
        for k in range(2):
            greet(root, relay_of(k))
        pl.semaphore_wait(barrier, n_sub + 3)

    @pl.when(rel == 2)
    def _():
        pl.semaphore_wait(barrier, n_sub - 1)

    @pl.when((rel == 1) | (rel == 3))
    def _():
        greet(root, relay_of(side))
        greet((sub + 1 + 2 * side) % n_sub, twin_blk)
        greet(sub, twin_blk)
        pl.semaphore_wait(barrier, n_sub + 2)

    def col_range(t):
        return pl.ds(pl.multiple_of((blk + t) % n_blk * items, items), items)

    def own_copies(t, slot):
        return (pltpu.make_async_copy(ratings.at[:, col_range(t)], rating_buf.at[slot, pl.ds(0, n_dev)], own_sem.at[slot]),
                pltpu.make_async_copy(mask.at[:, col_range(t)], mask_buf.at[slot], mask_sem.at[slot]))

    def load_own(t, slot):
        for copy in own_copies(t, slot):
            copy.start()

    def merge_own(t, slot):
        for copy in own_copies(t, slot):
            copy.wait()
        rating_buf[slot, pl.ds(0, n_dev)] = jnp.where(mask_buf[slot] != 0, rating_buf[slot, pl.ds(0, n_dev)], jnp.inf)

    def buf_rows(h, start, size):
        return rating_buf.at[h % 2, pl.ds(pl.multiple_of(h % DEPTH // 2 * 2 * n + start, half // 2), size)]

    def mask_rows(h):
        return mask_buf.at[h % 2, pl.ds(pl.multiple_of(h % DEPTH // 2 * n, n), n)]

    def part_copies(h):
        rows = pl.ds(pl.multiple_of(h % PARTS * n, n), n)
        return (pltpu.make_async_copy(ratings.at[rows, col_range(h // PARTS)], buf_rows(h, 0, n), own_sem.at[h % DEPTH]),
                pltpu.make_async_copy(mask.at[rows, col_range(h // PARTS)], mask_rows(h), mask_sem.at[h % DEPTH]))

    def load_part(h):
        for copy in part_copies(h):
            copy.start()

    def merge_part(h):
        for copy in part_copies(h):
            copy.wait()
        buf_rows(h, n, n)[...] = jnp.where(mask_rows(h)[...] != 0, buf_rows(h, 0, n)[...], jnp.inf)

    n_parts = n_blk * PARTS

    def side_rows(k, p):
        return pl.ds(n_dev + (2 * p + k) * region, n)

    def far_rows_of(k, p):
        return pl.ds(n_dev + (2 * p + k) * region + n, half)

    @pl.when(rel == 2)
    def _():
        for h in range(DEPTH):
            load_part(h)
        first = [remote(user_in.at[pl.ds(p * n + k * half, half)], user_st.at[far_rows_of(k, p)], user_send.at[k + 2 * p],
                        user_recv.at[2 + k, p], side_sub(k), blk) for p in range(PARTS) for k in range(2)]
        for copy in first:
            copy.start()

        def sends(h):
            return [remote(buf_rows(h, n + k * half, half), far_ratings.at[h, pl.ds(k * region + n, half)],
                           rating_send.at[h % DEPTH, k], far_recv.at[h], side_sub(k), blk) for k in range(2)]

        def turn(h, carry):
            @pl.when(h >= DEPTH)
            def _():
                for copy in sends(h - DEPTH):
                    copy.wait_send()
            merge_part(h)
            for copy in sends(h):
                copy.start()

            @pl.when(h + DEPTH < n_parts)
            def _():
                load_part(h + DEPTH)
            return carry

        lax.fori_loop(0, n_parts, turn, 0)
        for h in range(n_parts - DEPTH, n_parts):
            for copy in sends(h):
                copy.wait_send()
        for copy in first:
            copy.wait_send()
        for p in range(PARTS):
            for k in range(2):
                arrived(user_out.at[pl.ds(p * n + k * half, half)], out_recv.at[2 * p + k])
        for c in range(n_chunks):
            arrived(item_out.at[c], last_recv.at[c])

    def run_side(is_hot):
        for h in range(DEPTH):
            load_part(h)
        base = side * region

        def user_rows(p, start, size):
            return user_st.at[pl.ds(pl.multiple_of(n_dev + 2 * p * region + base + start, half), size)]

        mine = [remote(user_in.at[pl.ds(p * n, n)], user_rows(p, 0, n), user_send.at[p], user_recv.at[side, p], root, blk) for p in range(PARTS)]
        for copy in mine:
            copy.start()
        direct = direct_hot if is_hot else direct_cold
        passed_on = direct_cold if is_hot else direct_hot
        relay = relay_of(side)

        def rows(start, size):
            return pl.ds(pl.multiple_of(base + start, half // 2), size)

        def cuts(lo, hi):
            if lo < direct < hi:
                return [(lo, direct), (direct, hi)]
            return [(lo, hi)]

        def to_root_or_relay(src, h, lo, hi, sem):
            if hi <= direct:
                return remote(src, far_ratings.at[h, rows(lo, hi - lo)], sem, rating_recv.at[h], root, blk)
            return remote(src, far_ratings.at[n_parts + h, rows(lo, hi - lo)], sem, relay_recv.at[h], root, relay)

        def own_sends(h):
            return [to_root_or_relay(buf_rows(h, n + lo, hi - lo), h, lo, hi, rating_send.at[h % DEPTH, i])
                    for i, (lo, hi) in enumerate(cuts(0, n))]

        def far_sends(h):
            return [to_root_or_relay(far_ratings.at[h, rows(lo, hi - lo)], h, lo, hi, fwd_send.at[h % DEPTH, i])
                    for i, (lo, hi) in enumerate(cuts(n, region))]

        def relay_send(h):
            there = rows(passed_on, region - passed_on)
            return remote(far_ratings.at[n_parts + h, there], far_ratings.at[h, there], relay_sem.at[h % DEPTH], rating_recv.at[h], sub, twin_blk)

        def relay_turn(h):
            @pl.when(h >= DEPTH)
            def _():
                relay_send(h - DEPTH).wait_send()
            there = rows(passed_on, region - passed_on)
            arrived(far_ratings.at[n_parts + h, there], relay_recv.at[h])
            relay_send(h).start()

        passed = []
        for p in range(PARTS):
            arrived(user_rows(p, n, half), user_recv.at[2 + side, p])
            passed.append(remote(user_rows(p, n, half), user_rows(p, n, half), user_send.at[2 + p], user_recv.at[2 + side, p], root, blk))
            passed[-1].start()

        def turn(h, carry):
            @pl.when(h >= DEPTH)
            def _():
                for copy in own_sends(h - DEPTH) + far_sends(h - DEPTH):
                    copy.wait_send()
            merge_part(h)
            for copy in own_sends(h):
                copy.start()
            arrived(far_ratings.at[h, rows(n, half)], far_recv.at[h])
            for copy in far_sends(h):
                copy.start()

            @pl.when(h + DEPTH < n_parts)
            def _():
                load_part(h + DEPTH)

            @pl.when(h >= LAG)
            def _():
                relay_turn(h - LAG)
            return carry

        lax.fori_loop(0, n_parts, turn, 0)
        for h in range(n_parts - LAG, n_parts):
            relay_turn(h)
        for h in range(n_parts - DEPTH, n_parts):
            for copy in own_sends(h) + far_sends(h) + [relay_send(h)]:
                copy.wait_send()
        for copy in mine + passed:
            copy.wait_send()

    @pl.when(((rel == 1) | (rel == 3)) & hot)
    def _():
        run_side(True)

    @pl.when(((rel == 1) | (rel == 3)) & jnp.logical_not(hot))
    def _():
        run_side(False)

    @pl.when((rel == 1) | (rel == 3))
    def _():
        far = (root + 2) % n_sub
        backs = []
        for p in range(PARTS):
            arrived(user_st.at[pl.ds(p * half, half)], out_recv.at[2 + p])
            backs.append(remote(user_st.at[pl.ds(p * half, half)], user_out.at[pl.ds(pl.multiple_of(p * n + side * half, half), half)],
                                out_send.at[p], out_recv.at[2 * p + side], far, blk))
            backs[-1].start()
        for p in range(PARTS):
            arrived(user_out.at[pl.ds(p * n, n)], out_recv.at[p])
        back_items = []
        for c in range(n_chunks):
            arrived(item_out.at[c], last_recv.at[c])
            copy = remote(item_out.at[c], item_out.at[c], last_send.at[c], last_recv.at[c], far, blk)
            mine_to_pass = side == (2 * c) // n_chunks

            @pl.when(mine_to_pass)
            def _():
                copy.start()
            back_items.append((copy, mine_to_pass))
        for copy, mine_to_pass in back_items:
            @pl.when(mine_to_pass)
            def _():
                copy.wait_send()
        for copy in backs:
            copy.wait_send()

    @pl.when(rel == 0)
    def _():
        load_own(0, 0)
        for c in range(n_chunks):
            item_st[0, c] = item_in[c]
        user_st[pl.ds(0, n_dev)] = user_in[...]
        for k in range(2):
            for p in range(PARTS):
                arrived(user_st.at[side_rows(k, p)], user_recv.at[k, p])
                arrived(user_st.at[far_rows_of(k, p)], user_recv.at[2 + k, p])
        user_half[...] = user_st[...].astype(BF16)

        def root_copies(t, slot):
            return [pltpu.make_async_copy(far_ratings.at[t % n_blk * PARTS + p], rating_buf.at[slot, pl.ds(n_dev + 2 * p * region, 2 * region)],
                                          part_sem.at[slot, p]) for p in range(PARTS)]

        def item_copy(t, c):
            return remote(item_st.at[t, c], item_st.at[t + 1, c], item_send.at[c], item_recv.at[t + 1, c], root_of(next_blk), next_blk)

        def step(t, slot, first, last):
            for c in range(n_chunks):
                if first:
                    @pl.when(t > 0)
                    def _():
                        arrived(item_st.at[t, c], item_recv.at[t, c])
                cols = pl.ds(c * width, width)
                item_old = item_st[t, c]
                item_now = item_old.astype(BF16)
                item_half[:, cols] = item_now
                predicted = jnp.dot(user_half[...], item_now, preferred_element_type=F32)
                rating = rating_buf[slot, :, cols]
                err = jnp.where(rating == jnp.inf, 0.0, predicted - rating).astype(BF16)
                err_buf[:, cols] = err
                grad_item = lax.dot_general(user_half[...], err, (((0,), (0,)), ((), ())), preferred_element_type=F32)
                item_st[t, c] = item_old - step_size * (grad_item + decay_coef * item_old)
                if last:
                    item_copy(t, c).start()
            for i in range(users // USER_CHUNK):
                rows = pl.ds(i * USER_CHUNK, USER_CHUNK)
                grad_user = lax.dot_general(err_buf[rows, :], item_half[...], (((1,), (1,)), ((), ())), preferred_element_type=F32)
                user_old = user_st[rows, :]
                user_new = user_old - step_size * (grad_user + decay_coef * user_old)
                user_st[rows, :] = user_new
                user_half[rows, :] = user_new.astype(BF16)

        def turn(t, carry):
            slot = t % 2

            @pl.when(t < n_blk)
            def _():
                for p, copy in enumerate(root_copies(t, slot)):
                    arrived(far_ratings.at[t * PARTS + p], rating_recv.at[t * PARTS + p])
                    copy.start()
            merge_own(t, slot)
            for copy in root_copies(t, slot):
                copy.wait()

            @pl.when(t + 1 < n_turns)
            def _():
                load_own(t + 1, 1 - slot)

            @pl.when((t + 1 >= n_blk) & (t + 1 < n_turns))
            def _():
                for copy in root_copies(t + 1, 1 - slot):
                    copy.start()
            step(t, slot, True, False)

            def middle(_, c):
                step(t, slot, False, False)
                return c

            lax.fori_loop(0, STEPS - 2, middle, 0)

            @pl.when(t > 0)
            def _():
                for c in range(n_chunks):
                    item_copy(t - 1, c).wait_send()
            step(t, slot, False, True)
            return carry

        lax.fori_loop(0, n_turns, turn, 0)
        outs = []
        for p in range(PARTS):
            for k in range(2):
                outs.append(remote(user_st.at[far_rows_of(k, p)], user_st.at[pl.ds(p * half, half)], out_send.at[2 * p + k], out_recv.at[2 + p], side_sub(k), blk))
        for p in range(PARTS):
            for k in range(2):
                outs.append(remote(user_st.at[side_rows(k, p)], user_out.at[pl.ds(p * n, n)], out_send.at[4 + 2 * p + k], out_recv.at[p], side_sub(k), blk))
        for copy in outs:
            copy.start()
        user_out[...] = user_st[pl.ds(0, n_dev)]
        for c in range(n_chunks):
            arrived(item_st.at[n_turns, c], item_recv.at[n_turns, c])
            for k in range(2):
                copy = remote(item_st.at[n_turns, c], item_out.at[c], last_send.at[c + k * n_chunks], last_recv.at[c], side_sub(k), blk)
                copy.start()
                outs.append(copy)
            item_out[c] = item_st[n_turns, c]
        for c in range(n_chunks):
            item_copy(n_turns - 1, c).wait_send()
        for copy in outs:
            copy.wait_send()


def solution(mesh):
    n_sub, n_blk = mesh.shape['sub'], mesh.shape['blk']
    row_spec = P(('rep', 'blk', 'sub'), None)
    item_spec = P(('rep', 'blk'), None)

    def local_run(ratings, mask, user_init, item_init):
        users_dev = ratings.shape[0]
        items_dev, factor_dim = item_init.shape
        users = n_sub * users_dev
        big_side = max(items_dev, users)
        step_size = STEP_GAIN * math.sqrt(factor_dim) / (math.sqrt(big_side) + math.sqrt(factor_dim)) ** 2
        decay_coef = DECAY / step_size
        n_chunks = items_dev // ITEM_CHUNK
        n_turns = EPOCHS * n_blk
        item_parts = item_init.reshape(n_chunks, ITEM_CHUNK, factor_dim).transpose(0, 2, 1)
        hbm, vmem = pl.BlockSpec(memory_space=pltpu.HBM), pl.BlockSpec(memory_space=pltpu.VMEM)
        dma = pltpu.SemaphoreType.DMA
        user_out, item_out, _ = pl.pallas_call(
            functools.partial(kernel, n_sub, n_blk, step_size, decay_coef),
            out_shape=(jax.ShapeDtypeStruct(user_init.shape, F32), jax.ShapeDtypeStruct(item_parts.shape, F32),
                       jax.ShapeDtypeStruct((2 * n_blk * PARTS, (users - users_dev) // PARTS, items_dev), F32)),
            in_specs=[hbm, hbm, vmem, vmem],
            out_specs=(vmem, vmem, hbm),
            scratch_shapes=[
                pltpu.VMEM((2, users, items_dev), F32),
                pltpu.VMEM((2, users_dev, items_dev), jnp.int32),
                pltpu.VMEM((n_turns + 1,) + item_parts.shape, F32),
                pltpu.VMEM((users, factor_dim), F32),
                pltpu.VMEM((users, factor_dim), BF16),
                pltpu.VMEM((factor_dim, items_dev), BF16),
                pltpu.VMEM((users, items_dev), BF16),
                dma((DEPTH,)), dma((DEPTH,)), dma((2, PARTS)), dma((n_blk * PARTS,)), dma((n_blk * PARTS,)), dma((n_blk * PARTS,)), dma((DEPTH, 2)), dma((DEPTH, 2)), dma((DEPTH,)),
                dma((4, PARTS)), dma((2 * PARTS,)),
                dma((n_turns + 1, n_chunks)), dma((n_chunks,)), dma((2 * PARTS,)), dma((4 * PARTS,)), dma((n_chunks,)), dma((2 * n_chunks,)),
            ],
            compiler_params=pltpu.CompilerParams(collective_id=0, has_side_effects=True, vmem_limit_bytes=62 * 2**20),
            name='dsgd',
        )(ratings, mask, user_init, item_parts)
        return user_out, item_out.transpose(0, 2, 1).reshape(items_dev, factor_dim)

    return jax.shard_map(local_run, mesh=mesh, in_specs=(row_spec, row_spec, row_spec, item_spec), out_specs=(row_spec, item_spec), check_vma=False)
```

time: 614 us -> 532 us (0.87)
  Pallas kernels: 605 us -> 519 us
    pallas_call x1, Pallas kernels: 605 us -> 519 us  [local_run(): pl.pallas_call(functools.partial(kernel, n_sub, n_blk, step_size, decay_c...]
where the time goes in v2:
time: 532 us; the launch traced here: 527 us
  Pallas kernels  519 us (98%)
  local copies, waits for them, and re-layouts  6.93 us (1%)
    pallas_call x1, Pallas kernels, local_run(): pl.pallas_call(functools.partial(kernel, n_sub, n_blk, step_size, decay_c...  519 us

profile of v2, /device:TPU:112, one launch (start us, length us, event | category | flops | bytes accessed | tf_op | source)
XLA Modules:
  0.0 527.0 jit_solution(12962633672385883245)
XLA Ops:
  0.6 2.5 copy.6
  3.2 519.5 %dsgd.1 = (f32[512,256]{1,0:T(8,128)}, f32[4,256,256]{2,1,0:T(8,128)}, f32[32,768,1024]{2,1,0:T(8,128)}) custom-call(f32[512,8192]{1,0:T(8,128)} %ratings.1, s32[512,8192]{1,0:T(8,128)} %mask.1, f32[512,256]{1,0:T(8,128)} %user_in.1, f32[4,256,256]{2,1,0:T(8,128)} %bitcast.4), custom_call_target="tpu_custom_call" | custom-call | tf_op jit(solution)/shard_map/dsgd/pallas_call | solution.py:416
  522.6 2.5 copy.7
  525.2 1.9 copy.9

commit v3 on v2

--- a/solution.py
+++ b/solution.py
@@ -16,13 +16,14 @@
 PARTS = 2
 DEPTH = 4
 LAG = 1
+PIECES = 4
 F32 = jnp.float32
 BF16 = jnp.bfloat16
 
 
 def kernel(n_sub, n_blk, step_size, decay_coef, ratings, mask, user_in, item_in, user_out, item_out, far_ratings,
            rating_buf, mask_buf, item_st, user_st, user_half, item_half, err_buf,
-           own_sem, mask_sem, part_sem, rating_recv, far_recv, relay_recv, rating_send, fwd_send, relay_sem, user_recv, user_send, item_recv, item_send,
+           own_sem, mask_sem, part_sem, rating_recv, far_recv, relay_recv, rating_send, fwd_send, relay_sem, user_recv, user_send, item_recv, item_send, hop_recv, hop_send,
            out_recv, out_send, last_recv, last_send):
     rep, sub, blk = lax.axis_index('rep'), lax.axis_index('sub'), lax.axis_index('blk')
     n_dev = user_in.shape[0]
@@ -76,7 +77,9 @@
             greet(root_of(b), b)
         for k in range(2):
             greet(root, relay_of(k))
-        pl.semaphore_wait(barrier, n_sub + 3)
+        relay_side = 1 - prev_blk // 2 % 2
+        greet((root_of(prev_blk) + 1 + 2 * relay_side) % n_sub, prev_blk)
+        pl.semaphore_wait(barrier, n_sub + 4)
 
     @pl.when(rel == 2)
     def _():
@@ -87,7 +90,15 @@
         greet(root, relay_of(side))
         greet((sub + 1 + 2 * side) % n_sub, twin_blk)
         greet(sub, twin_blk)
-        pl.semaphore_wait(barrier, n_sub + 2)
+
+        @pl.when(hot)
+        def _():
+            greet(root_of(next_blk), next_blk)
+            pl.semaphore_wait(barrier, n_sub + 3)
+
+        @pl.when(jnp.logical_not(hot))
+        def _():
+            pl.semaphore_wait(barrier, n_sub + 2)
 
     def col_range(t):
         return pl.ds(pl.multiple_of((blk + t) % n_blk * items, items), items)
@@ -126,6 +137,7 @@
         buf_rows(h, n, n)[...] = jnp.where(mask_rows(h)[...] != 0, buf_rows(h, 0, n)[...], jnp.inf)
 
     n_parts = n_blk * PARTS
+    piece_rows = factor_dim // PIECES
 
     def side_rows(k, p):
         return pl.ds(n_dev + (2 * p + k) * region, n)
@@ -259,6 +271,25 @@
     @pl.when(((rel == 1) | (rel == 3)) & hot)
     def _():
         run_side(True)
+
+        def hop(t, i, q):
+            piece = item_st.at[t + 1, 2 * i + 1, pl.ds(q * piece_rows, piece_rows)]
+            return remote(piece, piece, hop_send.at[i, q], item_recv.at[t + 1, 2 * i + 1], root_of(next_blk), next_blk)
+
+        def hops(t, carry):
+            for i in range(n_chunks // 2):
+                for q in range(PIECES):
+                    @pl.when(t > n_blk)
+                    def _():
+                        hop(t - 1, i, q).wait_send()
+                    arrived(item_st.at[t + 1, 2 * i + 1, pl.ds(q * piece_rows, piece_rows)], hop_recv.at[t - n_blk, i, q])
+                    hop(t, i, q).start()
+            return carry
+
+        lax.fori_loop(n_blk, n_turns, hops, 0)
+        for i in range(n_chunks // 2):
+            for q in range(PIECES):
+                hop(n_turns - 1, i, q).wait_send()
 
     @pl.when(((rel == 1) | (rel == 3)) & jnp.logical_not(hot))
     def _():
@@ -327,8 +358,19 @@
                 err_buf[:, cols] = err
                 grad_item = lax.dot_general(user_half[...], err, (((0,), (0,)), ((), ())), preferred_element_type=F32)
                 item_st[t, c] = item_old - step_size * (grad_item + decay_coef * item_old)
-                if last:
+                if last and c % 2 == 0:
                     item_copy(t, c).start()
+                if last and c % 2 == 1:
+                    @pl.when(t < n_blk)
+                    def _():
+                        item_copy(t, c).start()
+
+                    @pl.when(t >= n_blk)
+                    def _():
+                        for q in range(PIECES):
+                            at = pl.ds(q * piece_rows, piece_rows)
+                            remote(item_st.at[t, c, at], item_st.at[t + 1, c, at], item_send.at[c], hop_recv.at[t - n_blk, c // 2, q],
+                                   side_sub(1 - col % 2), blk).start()
             for i in range(users // USER_CHUNK):
                 rows = pl.ds(i * USER_CHUNK, USER_CHUNK)
                 grad_user = lax.dot_general(err_buf[rows, :], item_half[...], (((1,), (1,)), ((), ())), preferred_element_type=F32)
@@ -429,7 +471,7 @@
                 pltpu.VMEM((users, items_dev), BF16),
                 dma((DEPTH,)), dma((DEPTH,)), dma((2, PARTS)), dma((n_blk * PARTS,)), dma((n_blk * PARTS,)), dma((n_blk * PARTS,)), dma((DEPTH, 2)), dma((DEPTH, 2)), dma((DEPTH,)),
                 dma((4, PARTS)), dma((2 * PARTS,)),
-                dma((n_turns + 1, n_chunks)), dma((n_chunks,)), dma((2 * PARTS,)), dma((4 * PARTS,)), dma((n_chunks,)), dma((2 * n_chunks,)),
+                dma((n_turns + 1, n_chunks)), dma((n_chunks,)), dma((n_blk, n_chunks // 2, PIECES)), dma((n_chunks // 2, PIECES)), dma((2 * PARTS,)), dma((4 * PARTS,)), dma((n_chunks,)), dma((2 * n_chunks,)),
             ],
             compiler_params=pltpu.CompilerParams(collective_id=0, has_side_effects=True, vmem_limit_bytes=62 * 2**20),
             name='dsgd',

time: 532 us -> 514 us (0.966)
  Pallas kernels: 519 us -> 506 us
    pallas_call x1, Pallas kernels: 519 us -> 506 us  [local_run(): pl.pallas_call(functools.partial(kernel, n_sub, n_blk, step_size, decay_c...]
where the time goes in v3:
time: 514 us; the launch traced here: 513 us
  Pallas kernels  506 us (98%)
  local copies, waits for them, and re-layouts  6.93 us (1%)
    pallas_call x1, Pallas kernels, local_run(): pl.pallas_call(functools.partial(kernel, n_sub, n_blk, step_size, decay_c...  506 us

profile of v3, /device:TPU:112, one launch (start us, length us, event | category | flops | bytes accessed | tf_op | source)
XLA Modules:
  0.0 513.3 jit_solution(6150531090500897887)
XLA Ops:
  0.6 2.5 copy.6
  3.2 505.8 %dsgd.1 = (f32[512,256]{1,0:T(8,128)}, f32[4,256,256]{2,1,0:T(8,128)}, f32[32,768,1024]{2,1,0:T(8,128)}) custom-call(f32[512,8192]{1,0:T(8,128)} %ratings.1, s32[512,8192]{1,0:T(8,128)} %mask.1, f32[512,256]{1,0:T(8,128)} %user_in.1, f32[4,256,256]{2,1,0:T(8,128)} %bitcast.4), custom_call_target="tpu_custom_call" | custom-call | tf_op jit(solution)/shard_map/dsgd/pallas_call | solution.py:458
  508.9 2.5 copy.7
  511.5 1.9 copy.9

commit v4 on v3

--- a/solution.py
+++ b/solution.py
@@ -16,7 +16,7 @@
 PARTS = 2
 DEPTH = 4
 LAG = 1
-PIECES = 4
+PIECES = 8
 F32 = jnp.float32
 BF16 = jnp.bfloat16
 

time: 514 us -> 512 us (level)
  no operation moved by 1% of the time
where the time goes in v4:
time: 512 us
  Pallas kernels  504 us (98%)
  local copies, waits for them, and re-layouts  6.93 us (1%)
    pallas_call x1, Pallas kernels, local_run(): pl.pallas_call(functools.partial(kernel, n_sub, n_blk, step_size, decay_c...  504 us

profile of v4, /device:TPU:112, one launch (start us, length us, event | category | flops | bytes accessed | tf_op | source)
XLA Modules:
  0.0 511.5 jit_solution(14369676682112681049)
XLA Ops:
  0.6 2.5 copy.6
  3.2 504.0 %dsgd.1 = (f32[512,256]{1,0:T(8,128)}, f32[4,256,256]{2,1,0:T(8,128)}, f32[32,768,1024]{2,1,0:T(8,128)}) custom-call(f32[512,8192]{1,0:T(8,128)} %ratings.1, s32[512,8192]{1,0:T(8,128)} %mask.1, f32[512,256]{1,0:T(8,128)} %user_in.1, f32[4,256,256]{2,1,0:T(8,128)} %bitcast.4), custom_call_target="tpu_custom_call" | custom-call | tf_op jit(solution)/shard_map/dsgd/pallas_call | solution.py:458
  507.1 2.5 copy.7
  509.7 1.9 copy.9
